TPU v7x, 256 devices: a whole 4x4x8 slice. The times are simulated.
256 devices in a mesh: dp: 256 (over y, x, z, core).
Axes of the slice: x: 4, y: 4, z: 8, core: 2. Of those that a mesh axis runs over, the one named last changes fastest.
Arguments:
- gradients: bfloat16 [256, 384, 4608], P('dp'), may hold values from -144 to 144
- owned_rows: int32 [256], replicated, may hold values from 1 to 3, 384 in all
- master: float32 [768, 4608], P('dp'), may hold values from -0.09375 to 0.09375
- first_moment: float32 [768, 4608], P('dp'), may hold values from -0.01171875 to 0.01171875
- second_moment: float32 [768, 4608], P('dp'), may hold values from 1.695421e-07 to 1.695421e-06
Outputs:
- new_master: float32 [768, 4608], P('dp')
- new_first: float32 [768, 4608], P('dp')
- new_second: float32 [768, 4608], P('dp')
- direction: float32 [768, 4608], P('dp')
- weights: bfloat16 [384, 4608], replicated
Inputs may be any that keep to these rules, and one draw needn't show every extreme that they name: `owned_rows`: owners hold consecutive flat rows in owner order; the counts sum to 384 and some owner holds exactly 3.
All inputs are finite; a program needn't handle non-finite values.
Results may differ from a plain program's by a relative error of at most 0.001.
Values may be sent and summed in bfloat16 or wider, within the bound.
A program may use at most 128 MiB of HBM per device.

v0:
```python
import jax
import jax.numpy as jnp
from jax import lax
from jax.sharding import PartitionSpec as P

CAP = 3
STEP = 100


beta_one = 0.9
beta_two = 0.999
adam_eps = 1e-08
learn_rate = 0.001
decay_rate = 0.1
clip_norm = 1.0


def table_lookup(table, positions):
    owners = jnp.arange(table.shape[0], dtype=jnp.int32)
    matches = positions[:, None] == owners[None, :]
    return jnp.sum(jnp.where(matches, table[None, :], 0), axis=1)


def slot_plan(owned_rows, row_starts, slot_list):
    owner_of = slot_list // CAP
    within_slot = slot_list % CAP
    live_mask = within_slot < table_lookup(owned_rows, owner_of)
    flat_rows = jnp.where(live_mask, table_lookup(row_starts, owner_of) + within_slot, 0)
    return (flat_rows, live_mask)


def per_device(gradients, owned_rows, master, first_moment, second_moment):
    local_grad = gradients[0]
    row_count = local_grad.shape[0]
    capacity = master.shape[0]
    row_starts = jnp.cumsum(owned_rows) - owned_rows
    my_index = lax.axis_index("dp")
    own_slots = my_index * capacity + jnp.arange(capacity, dtype=jnp.int32)
    own_rows, own_live = slot_plan(owned_rows, row_starts, own_slots)
    live_rows = own_live[:, None]
    summed = lax.psum(local_grad.astype(jnp.float32), "dp")
    norm_sq = jnp.sum(summed * summed)
    own_grad = jnp.where(live_rows, summed[own_rows], 0.0)
    clip_scale = jnp.minimum(1.0, clip_norm / (jnp.sqrt(norm_sq) + 1e-06))
    slot_grad = own_grad * clip_scale
    new_first = beta_one * first_moment + (1.0 - beta_one) * slot_grad
    new_second = beta_two * second_moment + (1.0 - beta_two) * slot_grad * slot_grad
    first_hat = new_first / (1.0 - beta_one**STEP)
    second_hat = new_second / (1.0 - beta_two**STEP)
    direction = first_hat / (jnp.sqrt(second_hat) + adam_eps) + decay_rate * master
    new_master = master - learn_rate * direction
    new_master = jnp.where(live_rows, new_master, 0.0)
    new_first = jnp.where(live_rows, new_first, 0.0)
    new_second = jnp.where(live_rows, new_second, 0.0)
    direction = jnp.where(live_rows, direction, 0.0)
    gathered = lax.all_gather(new_master.astype(jnp.bfloat16), "dp", axis=0, tiled=True)
    row_list = jnp.arange(row_count, dtype=jnp.int32)
    row_owner = jnp.sum((row_starts[None, :] <= row_list[:, None]).astype(jnp.int32), axis=1) - 1
    row_slot = row_owner * capacity + row_list - table_lookup(row_starts, row_owner)
    weights = gathered[row_slot]
    return (new_master, new_first, new_second, direction, weights)


def solution(mesh):
    in_specs = (P("dp", None, None), P(), P("dp", None), P("dp", None), P("dp", None))
    out_specs = (P("dp", None), P("dp", None), P("dp", None), P("dp", None), P())
    return jax.shard_map(
        per_device, mesh=mesh, in_specs=in_specs, out_specs=out_specs, check_vma=False
    )
```

profile of v0, /device:TPU:1, one launch (start us, length us, event | category | flops | bytes accessed | tf_op | source)
XLA Modules:
  0.0 456.9 jit_solution(313930386242864864)
XLA Ops:
  7.2 0.0 copy-start.3
  7.2 0.0 all-reduce.2.cloned.1.call-start
  7.2 5.8 %bitcast_convert_fusion = f32[384,4608]{1,0:T(8,128)} fusion(bf16[1,384,4608]{2,1,0:T(8,128)(2,1)} %param.5), kind=kLoop, calls=%fused_computation.3 | loop fusion | flops 1769472 | bytes 10616832 | tf_op jit(solution)/shard_map/convert_element_type | solution.py:41
  13.0 0.0 all-reduce.2.cloned.1.call-update
  13.1 0.0 all-gather.3.cloned.1.call-start
  13.1 0.0 copy-done.3
  13.1 0.3 reduce-window.9
  13.4 0.1 slice.7
  13.6 0.1 slice_reduce_fusion
  13.7 0.1 bitcast_subtract_fusion
  13.8 0.2 select_reduce_fusion.2
  14.0 278.4 %all-reduce.2.cloned.1.call-done = f32[384,4608]{1,0:T(8,128)} async-done(((f32[384,4608]{1,0:T(8,128)}), f32[384,4608]{1,0:T(8,128)}) %all-reduce.2.cloned.1.call-update) | async-done | bytes 7077904 | tf_op jit(solution)/shard_map/psum | solution.py:41
  292.4 5.4 %multiply_reduce_fusion = f32[]{:T(128)} fusion(f32[384,4608]{1,0:T(8,128)} %all-reduce.2.cloned.1.call-done), kind=kLoop, calls=%fused_computation.2 | loop fusion | flops 3538943 | bytes 7077892 | tf_op jit(solution)/shard_map/reduce_sum | solution.py:42
  298.6 3.6 gather_fusion
  302.2 0.0 copy-done
  302.2 0.0 copy-done.1
  302.2 0.9 convert_bitcast_fusion
  303.2 0.0 all-gather.3.cloned.1.call-update
  303.2 0.1 convert_reduce_fusion
  303.3 0.2 select_reduce_fusion
  303.6 0.7 broadcast_select_fusion
  304.3 118.3 %all-gather.3.cloned.1.call-done = bf16[256,3,4608]{2,1,0:T(4,128)(2,1)} async-done(((bf16[1,3,4608]{2,1,0:T(4,128)(2,1)}), bf16[256,3,4608]{2,1,0:T(4,128)(2,1)}) %all-gather.3.cloned.1.call-update) | async-done | bytes 7077904 | tf_op jit(solution)/shard_map/all_gather | solution.py:56
  422.6 14.3 %reshape.150 = bf16[768,4608]{1,0:T(8,128)(2,1)} reshape(bf16[256,3,4608]{2,1,0:T(4,128)(2,1)} %all-gather.3.cloned.1.call-done) | data formatting | bytes 14155776
  437.0 13.1 %gather_fusion.1 = bf16[384,4608]{1,0:T(8,128)(2,1)} fusion(bf16[768,4608]{1,0:T(8,128)(2,1)} %reshape.150, s32[1024]{0:T(1024)S(1)} %pad_clamp_fusion), kind=kCustom, calls=%fused_computation.1 | custom fusion | bytes 7079424 | tf_op jit(solution)/shard_map/gather | solution.py:60
  (12 shorter events, 0.1 us)
Async XLA Ops:
  7.2 6.0 %copy-start.3 = (s32[256]{0:T(256)S(1)}, s32[256]{0:T(256)}, u32[]{:S(2)}) copy-start(s32[256]{0:T(256)} %param.6) | copy-start | bytes 3076
  7.2 285.2 %all-reduce.2.cloned.1.call-start = ((), (), s32[]{:S(2)}) async-start(), calls=%async_computation | async-start | bytes 14155776 | tf_op jit(solution)/shard_map/psum | solution.py:41
  13.0 289.2 %copy-start = (f32[3,4608]{1,0:T(4,128)S(1)}, f32[3,4608]{1,0:T(4,128)}, u32[]{:S(2)}) copy-start(f32[3,4608]{1,0:T(4,128)} %param.7) | copy-start | bytes 165892
  13.0 289.2 %copy-start.1 = (f32[3,4608]{1,0:T(4,128)S(1)}, f32[3,4608]{1,0:T(4,128)}, u32[]{:S(2)}) copy-start(f32[3,4608]{1,0:T(4,128)} %param.9) | copy-start | bytes 165892
  13.0 289.2 %copy-start.2 = (f32[3,4608]{1,0:T(4,128)S(1)}, f32[3,4608]{1,0:T(4,128)}, u32[]{:S(2)}) copy-start(f32[3,4608]{1,0:T(4,128)} %param.8) | copy-start | bytes 165892
  13.1 409.5 %all-gather.3.cloned.1.call-start = ((), (), s32[]{:S(2)}) async-start(), calls=%async_computation.1 | async-start | bytes 9474048 | tf_op jit(solution)/shard_map/all_gather | solution.py:56
Sparse Core Ops, SparseCore 0:
  13.6 278.7 all-reduce.1
  303.3 119.2 all-gather.2
where the time goes:
time: 457 us
  waiting for transfers between devices  397 us (87%)
  local copies, waits for them, and re-layouts  31.3 us (7%)
  between operations  14.9 us (3%)
  other arithmetic  14 us (3%)
    psum x1, waiting for transfers between devices, per_device(): summed = lax.psum(local_grad.astype(jnp.float32), 'dp')  278 us
    all_gather x1, waiting for transfers between devices, per_device(): lax.all_gather(new_master.astype(jnp.bfloat16), 'dp', axis=0, tiled=True)  118 us
    unnamed x9, local copies, waits for them, and re-layouts  14.4 us
    gather x1, local copies, waits for them, and re-layouts, per_device(): weights = gathered[row_slot]  13.1 us
  transfers between devices with their start and end apart: 2, of which 2 were waited for; matrix products, arithmetic and copies ran while one was open for 0% of the time, Pallas kernels for 0%

commit v1 on v0

v1 whole, which is shorter than its diff:
```python
import jax
import jax.numpy as jnp
from jax import lax
from jax.experimental import pallas as pl
from jax.experimental.pallas import tpu as pltpu
from jax.sharding import PartitionSpec as P

CAP = 3
STEP = 100

beta_one = 0.9
beta_two = 0.999
adam_eps = 1e-08
learn_rate = 0.001
decay_rate = 0.1
clip_norm = 1.0

ROWS = 384
WIDTH = 4608
HALF_TILES = 18
CHUNK = 640
SLOTS = 1024
ORDER = (2, 1, 3, 0)
OWN_TILES = (4, 5, 4, 5)

MESH = pl.DeviceIdType.MESH
f32 = jnp.float32
bf16 = jnp.bfloat16


def window_start(k):
    return (9 * k) // 2


def kernel(
    grad,
    owned,
    master,
    first,
    second,
    new_master,
    new_first,
    new_second,
    direction,
    weights,
    out_buf,
    own_buf,
    pair_buf,
    p_far,
    p_dir,
    p_mid,
    p_com,
    base,
    put,
    take,
    slot_buf,
    q_far,
    q_dir,
    q_mid,
    q_com,
    z_own,
    z_got,
    done_buf,
    norm_one,
    norm_two,
    norm_own,
    norm_mid,
    mine,
    grad_buf,
    w_full,
    w_send,
    w_got,
    e_all,
    flat_own,
    flat_pair,
    load_sem,
    pair_send,
    pair_recv,
    p_send,
    p_recv,
    q_send,
    q_recv,
    z_send,
    z_recv,
    t_send,
    t_recv,
    n1_send,
    n1_recv,
    n2_send,
    n2_recv,
    u_send,
    u_recv,
    zg_send,
    zg_recv,
    qg_send,
    qg_recv,
    pg_send,
    pg_recv,
    c_send,
    c_recv,
    out_sem,
):
    me = lax.axis_index("dp")
    y, x, z, c = me // 64, (me // 16) % 4, (me // 2) % 8, me % 2
    p = x + c * (y - x)
    q = y + c * (x - y)
    p_step = 16 + 48 * c
    q_step = 64 - 48 * c
    line, plane = me % 16, me // 16
    other = me + 1 - 2 * c

    def at_p(v):
        return me + (v - p) * p_step

    def at_q(v):
        return me + (v - q) * q_step

    def at_line(v):
        return me - line + v

    def at_plane(v):
        return v * 16 + line

    sends = []

    def send(src, dst, ssem, rsem, dev):
        copy = pltpu.make_async_remote_copy(
            src_ref=src, dst_ref=dst, send_sem=ssem, recv_sem=rsem,
            device_id=(dev,), device_id_type=MESH,
        )
        copy.start()
        sends.append(copy)

    def got(dst, ssem, rsem):
        pltpu.make_async_remote_copy(
            src_ref=dst, dst_ref=dst, send_sem=ssem, recv_sem=rsem,
            device_id=(other,), device_id_type=MESH,
        ).wait_recv()

    def columns(color, k):
        start = pl.multiple_of((HALF_TILES * color + window_start(k)) * 128, 128)
        return pl.ds(start, CHUNK)

    loads = {}
    for n, j in enumerate(ORDER):
        loads["out", j] = pltpu.make_async_copy(
            grad.at[0, :, columns(1 - c, (q + j) % 4)], out_buf.at[j], load_sem.at[n])
        loads["own", j] = pltpu.make_async_copy(
            grad.at[0, :, columns(c, (p + j) % 4)], own_buf.at[j], load_sem.at[4 + n])
    for j in ORDER:
        loads["out", j].start()
    for j in ORDER:
        loads["own", j].start()

    barrier = pltpu.get_barrier_semaphore()
    peers = [at_line((line + d) % 16) for d in range(1, 16)]
    peers += [at_plane((plane + d) % 16) for d in range(1, 16)]
    peers += [at_p((p + d) % 4) + 1 - 2 * c for d in range(1, 4)]
    peers += [at_q((q + d) % 4) + 1 - 2 * c for d in range(1, 4)]
    for dev in peers:
        pl.semaphore_signal(barrier, inc=1, device_id=(dev,), device_id_type=MESH)
    pl.semaphore_wait(barrier, len(peers))

    for j in ORDER:
        loads["out", j].wait()
        send(out_buf.at[j], pair_buf.at[j], pair_send.at[j], pair_recv.at[j], other)

    counts = owned[...].astype(f32)

    def owner_of(s):
        qq, zz, pp, cc = s // 256, (s // 32) % 8, (s // 8) % 4, (s // 4) % 2
        yy = qq + c * (pp - qq)
        xx = pp + c * (qq - pp)
        return yy * 64 + xx * 16 + zz * 2 + cc

    def put_step(i, carry):
        s = i * 128 + lax.broadcasted_iota(jnp.int32, (128, 256), 0)
        owner = owner_of(s)
        lane = lax.broadcasted_iota(jnp.int32, (128, 256), 1)
        count = jnp.sum(jnp.where(lane == owner, counts, 0.0), axis=1, keepdims=True)
        start = jnp.sum(jnp.where(lane < owner, counts, 0.0), axis=1, keepdims=True)
        slot = (lax.broadcasted_iota(jnp.int32, (128, 1), 0) % 4).astype(f32)
        row = jnp.where(slot < count, start + slot, -1.0)
        flat = lax.broadcasted_iota(jnp.int32, (128, ROWS), 1).astype(f32)
        put[pl.ds(pl.multiple_of(i * 128, 128), 128), :] = jnp.where(row == flat, 1.0, 0.0).astype(bf16)
        return carry

    lax.fori_loop(0, SLOTS // 128, put_step, 0)

    for i in range(4):
        s = i * 256 + lax.broadcasted_iota(jnp.int32, (256, 256), 1)
        owner = owner_of(s)
        holder = lax.broadcasted_iota(jnp.int32, (256, 256), 0)
        same = jnp.where(holder == owner, 1.0, 0.0).astype(bf16)
        earlier = jnp.where(holder < owner, 1.0, 0.0).astype(bf16)
        lhs = jnp.broadcast_to(counts, (8, 256)).astype(bf16)
        count = jnp.dot(lhs, same, preferred_element_type=f32)[0:1]
        start = jnp.dot(lhs, earlier, preferred_element_type=f32)[0:1]
        slot = (lax.broadcasted_iota(jnp.int32, (1, 256), 1) % 4).astype(f32)
        row = jnp.where(slot < count, start + slot, -1.0)
        flat = lax.broadcasted_iota(jnp.int32, (ROWS, 256), 0).astype(f32)
        take[:, i * 256:(i + 1) * 256] = jnp.where(row == flat, 1.0, 0.0).astype(bf16)

    def rows_add(dst, dst_at, terms, count, step=32):
        def body(i, carry):
            total = None
            for ref, at in terms:
                part = ref[pl.ds(pl.multiple_of(at + i * step, step), step), :].astype(f32)
                total = part if total is None else total + part
            dst[pl.ds(pl.multiple_of(dst_at + i * step, step), step), :] = total.astype(dst.dtype)
            return carry
        lax.fori_loop(0, count // step, body, 0)

    def ring_reduce(acc, half, prepare, far, direct, mid, com, ssem, rsem, nxt, prv, finish):
        lo, hi = pl.ds(0, half), pl.ds(half, half)
        prepare(2)
        send(acc.at[2, lo], far.at[0], ssem.at[0], rsem.at[0], nxt)
        send(acc.at[2, hi], far.at[1], ssem.at[1], rsem.at[1], prv)
        prepare(1)
        send(acc.at[1, hi], direct.at[1], ssem.at[2], rsem.at[2], nxt)
        prepare(3)
        send(acc.at[3, lo], direct.at[0], ssem.at[3], rsem.at[3], prv)
        prepare(0)
        got(far.at[0], ssem.at[0], rsem.at[0])
        rows_add(mid.at[0], 0, [(acc.at[1], 0), (far.at[0], 0)], half)
        send(mid.at[0], com.at[0], ssem.at[4], rsem.at[4], nxt)
        got(far.at[1], ssem.at[1], rsem.at[1])
        rows_add(mid.at[1], 0, [(acc.at[3], half), (far.at[1], 0)], half)
        send(mid.at[1], com.at[1], ssem.at[5], rsem.at[5], prv)
        got(direct.at[0], ssem.at[3], rsem.at[3])
        got(direct.at[1], ssem.at[2], rsem.at[2])
        got(com.at[0], ssem.at[4], rsem.at[4])
        rows_add(finish, 0, [(acc.at[0], 0), (direct.at[0], 0), (com.at[0], 0)], half)
        got(com.at[1], ssem.at[5], rsem.at[5])
        rows_add(finish, half, [(acc.at[0], half), (direct.at[1], 0), (com.at[1], 0)], half)

    def pair_prepare(j):
        loads["own", j].wait()
        got(pair_buf.at[j], pair_send.at[j], pair_recv.at[j])
        rows_add(own_buf.at[j], 0, [(own_buf.at[j], 0), (pair_buf.at[j], 0)], ROWS)

    ring_reduce(own_buf, 192, pair_prepare, p_far, p_dir, p_mid, p_com, p_send, p_recv,
                at_p((p + 1) % 4), at_p((p + 3) % 4), base)

    def slot_prepare(j):
        at = ((q + j) % 4) * 256
        def body(i, carry):
            rows = put[pl.ds(pl.multiple_of(at + i * 128, 128), 128), :]
            picked = jnp.dot(rows, base[...], preferred_element_type=f32)
            slot_buf[j, pl.ds(pl.multiple_of(i * 128, 128), 128), :] = picked.astype(bf16)
            return carry
        lax.fori_loop(0, 2, body, 0)

    ring_reduce(slot_buf, 128, slot_prepare, q_far, q_dir, q_mid, q_com, q_send, q_recv,
                at_q((q + 1) % 4), at_q((q + 3) % 4), z_own)

    for d in range(1, 8):
        to = (z + d) % 8
        send(z_own.at[pl.ds(pl.multiple_of(to * 32, 32), 32)], z_got.at[d],
             z_send.at[d], z_recv.at[d], me + (to - z) * 2)
    total = z_own[pl.ds(pl.multiple_of(z * 32, 32), 32), :].astype(f32)
    for d in range(1, 8):
        got(z_got.at[d], z_send.at[d], z_recv.at[d])
        total = total + z_got[d].astype(f32)
    for k in range(4):
        done_buf[k] = total[8 * k:8 * k + 8]

    fifth = (p % 2).astype(f32)
    squares = total * total
    squares = squares[0:8] + squares[8:16] + squares[16:24] + squares[24:32]
    part = squares[:, 512:640] * fifth
    for k in range(4):
        part = part + squares[:, 128 * k:128 * k + 128]
    norm_own[...] = part
    for d in range(1, 16):
        send(norm_own, norm_one.at[d], n1_send.at[d], n1_recv.at[d], at_line((line + d) % 16))

    for core in range(2):
        for d in range(4):
            to = (p + d) % 4
            n = core * 4 + d
            dev = at_p(to) + core - c
            if d == 0:
                @pl.when(c != core)
                def _():
                    pltpu.make_async_remote_copy(
                        src_ref=done_buf.at[p], dst_ref=mine.at[c, p],
                        send_sem=t_send.at[n], recv_sem=t_recv.at[c, d],
                        device_id=(dev,), device_id_type=MESH).start()
            else:
                send(done_buf.at[to], mine.at[c, p], t_send.at[n], t_recv.at[c, d], dev)
    mine[c, p] = done_buf[p]

    for d in range(1, 16):
        got(norm_one.at[d], n1_send.at[d], n1_recv.at[d])
        part = part + norm_one[d]
    norm_mid[...] = part
    for d in range(1, 16):
        send(norm_mid, norm_two.at[d], n2_send.at[d], n2_recv.at[d], at_plane((plane + d) % 16))

    for color in range(2):
        for d in range(4):
            def wait(color=color, d=d):
                got(mine.at[0, 0], t_send.at[0], t_recv.at[color, d])
            if d == 0:
                pl.when(c != color)(wait)
            else:
                wait()
    for color in range(2):
        for k in range(4):
            at = (HALF_TILES * color + window_start(k)) * 128
            width = OWN_TILES[k] * 128
            grad_buf[:, at:at + width] = mine[color, k, :, 0:width]
    own_grad = jnp.where(c == 0, grad_buf[0:3, :], grad_buf[4:7, :])

    for d in range(1, 16):
        got(norm_two.at[d], n2_send.at[d], n2_recv.at[d])
        part = part + norm_two[d]
    norm_sq = jnp.sum(jnp.sum(part, axis=1, keepdims=True), axis=0, keepdims=True)
    clip_scale = jnp.minimum(1.0, clip_norm / (jnp.sqrt(norm_sq) + 1e-06))

    holders = lax.broadcasted_iota(jnp.int32, (1, 256), 1)
    my_count = jnp.sum(jnp.where(holders == me, counts, 0.0), axis=1, keepdims=True)
    live = lax.broadcasted_iota(jnp.int32, (3, WIDTH), 0).astype(f32) < my_count
    slot_grad = jnp.where(live, own_grad, 0.0) * clip_scale
    m = beta_one * first[...] + (1.0 - beta_one) * slot_grad
    v = beta_two * second[...] + (1.0 - beta_two) * slot_grad * slot_grad
    first_hat = m / (1.0 - beta_one**STEP)
    second_hat = v / (1.0 - beta_two**STEP)
    step = first_hat / (jnp.sqrt(second_hat) + adam_eps) + decay_rate * master[...]
    w = master[...] - learn_rate * step
    w = jnp.where(live, w, 0.0)
    new_master[...] = w
    new_first[...] = jnp.where(live, m, 0.0)
    new_second[...] = jnp.where(live, v, 0.0)
    direction[...] = jnp.where(live, step, 0.0)

    w_full[...] = jnp.zeros_like(w_full)

    @pl.when(c == 0)
    def _():
        w_full[0:3, :] = w

    @pl.when(c == 1)
    def _():
        w_full[4:7, :] = w

    for color in range(2):
        for k in range(4):
            at = (HALF_TILES * color + window_start(k)) * 128
            w_send[color, k] = w_full[:, at:at + CHUNK]
    for color in range(2):
        here = x if color == 0 else y
        stride = 16 if color == 0 else 64
        for d in range(4):
            to = (here + d) % 4
            n = color * 4 + d
            dev = me + (to - here) * stride + color - c
            if d == 0:
                @pl.when(c != color)
                def _():
                    pltpu.make_async_remote_copy(
                        src_ref=w_send.at[color, here], dst_ref=w_got.at[here, c],
                        send_sem=u_send.at[n], recv_sem=u_recv.at[c, d],
                        device_id=(dev,), device_id_type=MESH).start()
            else:
                send(w_send.at[color, to], w_got.at[here, c], u_send.at[n], u_recv.at[c, d], dev)
    w_got[p, c] = w_send[c, p]
    for core in range(2):
        for d in range(4):
            def wait(core=core, d=d):
                got(w_got.at[0, 0], u_send.at[0], u_recv.at[core, d])
            if d == 0:
                pl.when(c != core)(wait)
            else:
                wait()
    rows = jnp.concatenate([w_got[k, 0] + w_got[k, 1] for k in range(4)], axis=0)
    place = pl.multiple_of(q * 256 + z * 32, 32)
    e_all[pl.ds(place, 32), :] = rows.astype(bf16)

    for d in range(1, 8):
        to = (z + d) % 8
        send(e_all.at[pl.ds(place, 32)], e_all.at[pl.ds(place, 32)],
             zg_send.at[d], zg_recv.at[d], me + (to - z) * 2)
    for d in range(1, 8):
        came = pl.multiple_of(q * 256 + ((z + 8 - d) % 8) * 32, 32)
        got(e_all.at[pl.ds(came, 32)], zg_send.at[d], zg_recv.at[d])

    def ring_gather(part_of, pos, ssem, rsem, nxt, prv, after=None):
        def push(k, h, s, dev):
            send(part_of(k, h), part_of(k, h), ssem.at[s], rsem.at[s], dev)

        def come(k, h, s):
            got(part_of(k, h), ssem.at[s], rsem.at[s])

        push(pos, 0, 0, prv)
        push(pos, 1, 1, nxt)
        push(pos, 1, 2, prv)
        push(pos, 0, 3, nxt)
        if after is not None:
            after(pos)
        above, below, far = (pos + 1) % 4, (pos + 3) % 4, (pos + 2) % 4
        come(above, 0, 0)
        push(above, 0, 4, prv)
        come(below, 1, 1)
        push(below, 1, 5, nxt)
        come(above, 1, 2)
        if after is not None:
            after(above)
        come(below, 0, 3)
        if after is not None:
            after(below)
        come(far, 0, 4)
        come(far, 1, 5)
        if after is not None:
            after(far)

    ring_gather(lambda k, h: e_all.at[pl.ds(pl.multiple_of(k * 256 + h * 128, 128), 128)],
                q, qg_send, qg_recv, at_q((q + 1) % 4), at_q((q + 3) % 4))

    def take_step(i, carry):
        at = pl.multiple_of(i * 128, 128)
        picked = jnp.dot(take[pl.ds(at, 128), :], e_all[...], preferred_element_type=f32)
        flat_own[p, pl.ds(at, 128), :] = picked.astype(bf16)
        return carry

    lax.fori_loop(0, 3, take_step, 0)

    order = []

    def pass_on(k):
        n = len(order)
        order.append(k)
        send(flat_own.at[k], flat_pair.at[k], c_send.at[n], c_recv.at[n], other)

    ring_gather(lambda k, h: flat_own.at[k, pl.ds(h * 192, 192)],
                p, pg_send, pg_recv, at_p((p + 1) % 4), at_p((p + 3) % 4), pass_on)
    stores = []

    def store(buf, color, k, n):
        at = pl.multiple_of((HALF_TILES * color + window_start(k)) * 128, 128)
        width = OWN_TILES[k] * 128
        copy = pltpu.make_async_copy(
            buf.at[k, :, pl.ds(0, width)], weights.at[:, pl.ds(at, width)], out_sem.at[n])
        copy.start()
        stores.append(copy)

    for k in range(4):
        store(flat_own, c, k, k)
    for n, d in enumerate((0, 1, 3, 2)):
        got(flat_pair.at[(q + d) % 4], c_send.at[n], c_recv.at[n])
    for k in range(4):
        store(flat_pair, 1 - c, k, 4 + k)

    for copy in stores:
        copy.wait()
    for copy in sends:
        copy.wait_send()
    for core in range(2):
        @pl.when(c != core)
        def _():
            pltpu.make_async_remote_copy(
                src_ref=done_buf.at[0], dst_ref=mine.at[0, 0],
                send_sem=t_send.at[core * 4], recv_sem=t_recv.at[0, 0],
                device_id=(other,), device_id_type=MESH).wait_send()
            pltpu.make_async_remote_copy(
                src_ref=w_send.at[0, 0], dst_ref=w_got.at[0, 0],
                send_sem=u_send.at[core * 4], recv_sem=u_recv.at[0, 0],
                device_id=(other,), device_id_type=MESH).wait_send()


def per_device(gradients, owned_rows, master, first_moment, second_moment):
    vmem = pl.BlockSpec(memory_space=pltpu.VMEM)
    hbm = pl.BlockSpec(memory_space=pl.ANY)
    state = jax.ShapeDtypeStruct(master.shape, f32)
    dma = pltpu.SemaphoreType.DMA
    return pl.pallas_call(
        kernel,
        out_shape=(state, state, state, state, jax.ShapeDtypeStruct((ROWS, WIDTH), bf16)),
        in_specs=[hbm, vmem, vmem, vmem, vmem],
        out_specs=(vmem, vmem, vmem, vmem, hbm),
        scratch_shapes=[
            pltpu.VMEM((4, ROWS, CHUNK), bf16),
            pltpu.VMEM((4, ROWS, CHUNK), bf16),
            pltpu.VMEM((4, ROWS, CHUNK), bf16),
            pltpu.VMEM((2, 192, CHUNK), bf16),
            pltpu.VMEM((2, 192, CHUNK), bf16),
            pltpu.VMEM((2, 192, CHUNK), bf16),
            pltpu.VMEM((2, 192, CHUNK), bf16),
            pltpu.VMEM((ROWS, CHUNK), bf16),
            pltpu.VMEM((SLOTS, ROWS), bf16),
            pltpu.VMEM((ROWS, SLOTS), bf16),
            pltpu.VMEM((4, 256, CHUNK), bf16),
            pltpu.VMEM((2, 128, CHUNK), bf16),
            pltpu.VMEM((2, 128, CHUNK), bf16),
            pltpu.VMEM((2, 128, CHUNK), bf16),
            pltpu.VMEM((2, 128, CHUNK), bf16),
            pltpu.VMEM((256, CHUNK), bf16),
            pltpu.VMEM((8, 32, CHUNK), bf16),
            pltpu.VMEM((4, 8, CHUNK), f32),
            pltpu.VMEM((16, 8, 128), f32),
            pltpu.VMEM((16, 8, 128), f32),
            pltpu.VMEM((8, 128), f32),
            pltpu.VMEM((8, 128), f32),
            pltpu.VMEM((2, 4, 8, CHUNK), f32),
            pltpu.VMEM((8, WIDTH), f32),
            pltpu.VMEM((8, WIDTH), f32),
            pltpu.VMEM((2, 4, 8, CHUNK), f32),
            pltpu.VMEM((4, 2, 8, CHUNK), f32),
            pltpu.VMEM((SLOTS, CHUNK), bf16),
            pltpu.VMEM((4, ROWS, CHUNK), bf16),
            pltpu.VMEM((4, ROWS, CHUNK), bf16),
            dma((8,)),
            dma((4,)), dma((4,)),
            dma((6,)), dma((6,)),
            dma((6,)), dma((6,)),
            dma((8,)), dma((8,)),
            dma((8,)), dma((2, 4)),
            dma((16,)), dma((16,)),
            dma((16,)), dma((16,)),
            dma((8,)), dma((2, 4)),
            dma((8,)), dma((8,)),
            dma((6,)), dma((6,)),
            dma((6,)), dma((6,)),
            dma((4,)), dma((4,)),
            dma((8,)),
        ],
        compiler_params=pltpu.CompilerParams(
            collective_id=0, has_side_effects=True, vmem_limit_bytes=48 * 1024 * 1024),
    )(gradients, owned_rows.reshape(1, -1), master, first_moment, second_moment)


def solution(mesh):
    in_specs = (P("dp", None, None), P(), P("dp", None), P("dp", None), P("dp", None))
    out_specs = (P("dp", None), P("dp", None), P("dp", None), P("dp", None), P())
    return jax.shard_map(
        per_device, mesh=mesh, in_specs=in_specs, out_specs=out_specs, check_vma=False
    )
```

time: 457 us -> 102 us (0.22)
  waiting for transfers between devices: 397 us -> 0 us
  Pallas kernels: 0 us -> 93 us
  local copies, waits for them, and re-layouts: 31.3 us -> 7.65 us
  between operations: 14.9 us -> 0.65 us
  other arithmetic: 14 us -> 0 us
    psum x1 -> x0, waiting for transfers between devices: 278 us -> none  [per_device(): summed = lax.psum(local_grad.astype(jnp.float32), 'dp')]
    all_gather x1 -> x0, waiting for transfers between devices: 118 us -> none  [per_device(): lax.all_gather(new_master.astype(jnp.bfloat16), 'dp', axis=0, tiled=True)]
    pallas_call x0 -> x1, Pallas kernels: none -> 93 us  [per_device(): pl.pallas_call(kernel, out_shape=(state, state, state, state, jax.ShapeDt...]
    gather x2 -> x0, local copies, waits for them, and re-layouts: 16.8 us -> none  [the longest x1 13.1 us: per_device(): weights = gathered[row_slot]]
    unnamed x9 -> x13, local copies, waits for them, and re-layouts: 14.4 us -> 7.65 us
    reduce_sum x4 -> x0, other arithmetic: 5.99 us -> none  [the longest x1 5.43 us: per_device(): norm_sq = jnp.sum(summed * summed)]
    convert_element_type x1 -> x0, other arithmetic: 5.82 us -> none  [per_device(): summed = lax.psum(local_grad.astype(jnp.float32), 'dp')]
  transfers between devices with their start and end apart: 2 -> 0, of which waited for: 2 -> 0; matrix products, arithmetic and copies ran while one was open for 0% -> 0% of each run, Pallas kernels for 0% -> 0%
where the time goes in v1:
time: 102 us; the launch traced here: 101 us
  Pallas kernels  93 us (91%)
  local copies, waits for them, and re-layouts  7.65 us (8%)
    pallas_call x1, Pallas kernels, per_device(): pl.pallas_call(kernel, out_shape=(state, state, state, state, jax.ShapeDt...  93 us
    unnamed x13, local copies, waits for them, and re-layouts  7.65 us

profile of v1, /device:TPU:1, one launch (start us, length us, event | category | flops | bytes accessed | tf_op | source)
XLA Modules:
  0.0 101.3 jit_solution(13219835145403983550)
XLA Ops:
  0.6 0.0 copy-start
  0.6 0.9 copy-done
  1.5 0.0 copy-start.1
  1.5 0.9 copy-done.1
  2.4 0.0 copy-start.2
  2.4 0.9 copy-done.2
  3.3 0.0 copy-start.3
  3.3 0.7 copy-done.3
  4.0 93.0 %shard_map.92 = (f32[3,4608]{1,0:T(4,128)S(1)}, f32[3,4608]{1,0:T(4,128)S(1)}, f32[3,4608]{1,0:T(4,128)S(1)}, f32[3,4608]{1,0:T(4,128)S(1)}, bf16[384,4608]{1,0:T(8,128)(2,1)S(1)}) custom-call(bf16[1,384,4608]{2,1,0:T(8,128)(2,1)} %grad.1, s32[1,256]{1,0:T(1,128)S(1)} %bitcast.1, f32[3,4608]{1,0:T(4,128)S(1)} %copy-done, f32[3,4608]{1,0:T(4,128)S(1)} %copy-done.1, ...), custom_call_target="tpu_custom_call" | custom-call | tf_op jit(solution)/shard_map/pallas_call | solution.py:477
  97.0 0.6 copy.15
  97.6 0.6 copy.16
  98.3 0.6 copy.17
  98.9 0.6 copy.18
  99.5 1.8 %copy.19 = bf16[384,4608]{1,0:T(8,128)(2,1)} copy(bf16[384,4608]{1,0:T(8,128)(2,1)S(1)} %get-tuple-element.14) | data formatting | bytes 7077888
Async XLA Ops:
  0.6 0.9 copy-start
  1.5 0.9 copy-start.1
  2.4 0.9 copy-start.2
  3.3 0.7 copy-start.3

commit v2 on v1

--- a/solution.py
+++ b/solution.py
@@ -34,15 +34,20 @@
 
 def kernel(
     grad,
+    owned_hbm,
+    master_hbm,
+    first_hbm,
+    second_hbm,
+    new_master,
+    new_first,
+    new_second,
+    direction,
+    flat_own,
+    flat_pair,
     owned,
     master,
     first,
     second,
-    new_master,
-    new_first,
-    new_second,
-    direction,
-    weights,
     out_buf,
     own_buf,
     pair_buf,
@@ -67,12 +72,10 @@
     norm_mid,
     mine,
     grad_buf,
-    w_full,
-    w_send,
-    w_got,
+    s_full,
+    s_send,
+    s_got,
     e_all,
-    flat_own,
-    flat_pair,
     load_sem,
     pair_send,
     pair_recv,
@@ -98,7 +101,6 @@
     pg_recv,
     c_send,
     c_recv,
-    out_sem,
 ):
     me = lax.axis_index("dp")
     y, x, z, c = me // 64, (me // 16) % 4, (me // 2) % 8, me % 2
@@ -147,6 +149,13 @@
             grad.at[0, :, columns(1 - c, (q + j) % 4)], out_buf.at[j], load_sem.at[n])
         loads["own", j] = pltpu.make_async_copy(
             grad.at[0, :, columns(c, (p + j) % 4)], own_buf.at[j], load_sem.at[4 + n])
+    small = [
+        pltpu.make_async_copy(src, dst, load_sem.at[8 + n])
+        for n, (src, dst) in enumerate(
+            ((owned_hbm, owned), (master_hbm, master), (first_hbm, first), (second_hbm, second)))
+    ]
+    for copy in small:
+        copy.start()
     for j in ORDER:
         loads["out", j].start()
     for j in ORDER:
@@ -159,12 +168,8 @@
     peers += [at_q((q + d) % 4) + 1 - 2 * c for d in range(1, 4)]
     for dev in peers:
         pl.semaphore_signal(barrier, inc=1, device_id=(dev,), device_id_type=MESH)
-    pl.semaphore_wait(barrier, len(peers))
-
-    for j in ORDER:
-        loads["out", j].wait()
-        send(out_buf.at[j], pair_buf.at[j], pair_send.at[j], pair_recv.at[j], other)
-
+    for copy in small:
+        copy.wait()
     counts = owned[...].astype(f32)
 
     def owner_of(s):
@@ -201,6 +206,23 @@
         flat = lax.broadcasted_iota(jnp.int32, (ROWS, 256), 0).astype(f32)
         take[:, i * 256:(i + 1) * 256] = jnp.where(row == flat, 1.0, 0.0).astype(bf16)
 
+    s_full[...] = jnp.zeros_like(s_full)
+    for core in range(2):
+        @pl.when(c == core)
+        def _():
+            for a, ref in enumerate((master, first, second)):
+                s_full[8 * a + 4 * core:8 * a + 4 * core + 3, :] = ref[...]
+    for color in range(2):
+        for k in range(4):
+            at = (HALF_TILES * color + window_start(k)) * 128
+            s_send[color, k] = s_full[:, at:at + CHUNK]
+
+    pl.semaphore_wait(barrier, len(peers))
+
+    for j in ORDER:
+        loads["out", j].wait()
+        send(out_buf.at[j], pair_buf.at[j], pair_send.at[j], pair_recv.at[j], other)
+
     def rows_add(dst, dst_at, terms, count, step=32):
         def body(i, carry):
             total = None
@@ -212,27 +234,33 @@
         lax.fori_loop(0, count // step, body, 0)
 
     def ring_reduce(acc, half, prepare, far, direct, mid, com, ssem, rsem, nxt, prv, finish):
-        lo, hi = pl.ds(0, half), pl.ds(half, half)
+        part = half // 2
         prepare(2)
-        send(acc.at[2, lo], far.at[0], ssem.at[0], rsem.at[0], nxt)
-        send(acc.at[2, hi], far.at[1], ssem.at[1], rsem.at[1], prv)
+        for n in range(2):
+            piece = pl.ds(n * part, part)
+            send(acc.at[2, piece], far.at[0, piece], ssem.at[n], rsem.at[n], nxt)
+            send(acc.at[2, pl.ds(half + n * part, part)], far.at[1, piece], ssem.at[2 + n], rsem.at[2 + n], prv)
         prepare(1)
-        send(acc.at[1, hi], direct.at[1], ssem.at[2], rsem.at[2], nxt)
+        send(acc.at[1, pl.ds(half, half)], direct.at[1], ssem.at[4], rsem.at[4], nxt)
         prepare(3)
-        send(acc.at[3, lo], direct.at[0], ssem.at[3], rsem.at[3], prv)
+        send(acc.at[3, pl.ds(0, half)], direct.at[0], ssem.at[5], rsem.at[5], prv)
         prepare(0)
-        got(far.at[0], ssem.at[0], rsem.at[0])
-        rows_add(mid.at[0], 0, [(acc.at[1], 0), (far.at[0], 0)], half)
-        send(mid.at[0], com.at[0], ssem.at[4], rsem.at[4], nxt)
-        got(far.at[1], ssem.at[1], rsem.at[1])
-        rows_add(mid.at[1], 0, [(acc.at[3], half), (far.at[1], 0)], half)
-        send(mid.at[1], com.at[1], ssem.at[5], rsem.at[5], prv)
-        got(direct.at[0], ssem.at[3], rsem.at[3])
-        got(direct.at[1], ssem.at[2], rsem.at[2])
-        got(com.at[0], ssem.at[4], rsem.at[4])
-        rows_add(finish, 0, [(acc.at[0], 0), (direct.at[0], 0), (com.at[0], 0)], half)
-        got(com.at[1], ssem.at[5], rsem.at[5])
-        rows_add(finish, half, [(acc.at[0], half), (direct.at[1], 0), (com.at[1], 0)], half)
+        for n in range(2):
+            piece = pl.ds(n * part, part)
+            got(far.at[0, piece], ssem.at[n], rsem.at[n])
+            rows_add(mid.at[0], n * part, [(acc.at[1], n * part), (far.at[0], n * part)], part)
+            send(mid.at[0, piece], com.at[0, piece], ssem.at[6 + n], rsem.at[6 + n], nxt)
+            got(far.at[1, piece], ssem.at[2 + n], rsem.at[2 + n])
+            rows_add(mid.at[1], n * part, [(acc.at[3], half + n * part), (far.at[1], n * part)], part)
+            send(mid.at[1, piece], com.at[1, piece], ssem.at[8 + n], rsem.at[8 + n], prv)
+        got(direct.at[0], ssem.at[5], rsem.at[5])
+        got(direct.at[1], ssem.at[4], rsem.at[4])
+        for n in range(2):
+            piece = pl.ds(n * part, part)
+            got(com.at[0, piece], ssem.at[6 + n], rsem.at[6 + n])
+            rows_add(finish, n * part, [(acc.at[0], n * part), (direct.at[0], n * part), (com.at[0], n * part)], part)
+            got(com.at[1, piece], ssem.at[8 + n], rsem.at[8 + n])
+            rows_add(finish, half + n * part, [(acc.at[0], half + n * part), (direct.at[1], n * part), (com.at[1], n * part)], part)
 
     def pair_prepare(j):
         loads["own", j].wait()
@@ -258,6 +286,25 @@
         to = (z + d) % 8
         send(z_own.at[pl.ds(pl.multiple_of(to * 32, 32), 32)], z_got.at[d],
              z_send.at[d], z_recv.at[d], me + (to - z) * 2)
+
+    for color in range(2):
+        here = x if color == 0 else y
+        stride = 16 if color == 0 else 64
+        for d in range(4):
+            to = (here + d) % 4
+            n = color * 4 + d
+            dev = me + (to - here) * stride + color - c
+            if d == 0:
+                @pl.when(c != color)
+                def _():
+                    pltpu.make_async_remote_copy(
+                        src_ref=s_send.at[color, here], dst_ref=s_got.at[here, c],
+                        send_sem=u_send.at[n], recv_sem=u_recv.at[c, d],
+                        device_id=(dev,), device_id_type=MESH).start()
+            else:
+                send(s_send.at[color, to], s_got.at[here, c], u_send.at[n], u_recv.at[c, d], dev)
+    s_got[p, c] = s_send[c, p]
+
     total = z_own[pl.ds(pl.multiple_of(z * 32, 32), 32), :].astype(f32)
     for d in range(1, 8):
         got(z_got.at[d], z_send.at[d], z_recv.at[d])
@@ -298,6 +345,42 @@
     for d in range(1, 16):
         send(norm_mid, norm_two.at[d], n2_send.at[d], n2_recv.at[d], at_plane((plane + d) % 16))
 
+    for core in range(2):
+        for d in range(4):
+            def wait(core=core, d=d):
+                got(s_got.at[0, 0], u_send.at[0], u_recv.at[core, d])
+            if d == 0:
+                pl.when(c != core)(wait)
+            else:
+                wait()
+    states = [
+        jnp.concatenate([s_got[k, 0, 8 * a:8 * a + 8] + s_got[k, 1, 8 * a:8 * a + 8] for k in range(4)], axis=0)
+        for a in range(3)
+    ]
+
+    for d in range(1, 16):
+        got(norm_two.at[d], n2_send.at[d], n2_recv.at[d])
+        part = part + norm_two[d]
+    norm_sq = jnp.sum(jnp.sum(part, axis=1, keepdims=True), axis=0, keepdims=True)
+    clip_scale = jnp.minimum(1.0, clip_norm / (jnp.sqrt(norm_sq) + 1e-06))
+
+    def update(slot_grad, weight, moment, square):
+        m = beta_one * moment + (1.0 - beta_one) * slot_grad
+        v = beta_two * square + (1.0 - beta_two) * slot_grad * slot_grad
+        first_hat = m / (1.0 - beta_one**STEP)
+        second_hat = v / (1.0 - beta_two**STEP)
+        step = first_hat / (jnp.sqrt(second_hat) + adam_eps) + decay_rate * weight
+        return weight - learn_rate * step, m, v, step
+
+    rows, _, _, _ = update(total * clip_scale, *states)
+    place = pl.multiple_of(q * 256 + z * 32, 32)
+    e_all[pl.ds(place, 32), :] = rows.astype(bf16)
+
+    for d in range(1, 8):
+        to = (z + d) % 8
+        send(e_all.at[pl.ds(place, 32)], e_all.at[pl.ds(place, 32)],
+             zg_send.at[d], zg_recv.at[d], me + (to - z) * 2)
+
     for color in range(2):
         for d in range(4):
             def wait(color=color, d=d):
@@ -312,111 +395,57 @@
             width = OWN_TILES[k] * 128
             grad_buf[:, at:at + width] = mine[color, k, :, 0:width]
     own_grad = jnp.where(c == 0, grad_buf[0:3, :], grad_buf[4:7, :])
-
-    for d in range(1, 16):
-        got(norm_two.at[d], n2_send.at[d], n2_recv.at[d])
-        part = part + norm_two[d]
-    norm_sq = jnp.sum(jnp.sum(part, axis=1, keepdims=True), axis=0, keepdims=True)
-    clip_scale = jnp.minimum(1.0, clip_norm / (jnp.sqrt(norm_sq) + 1e-06))
-
     holders = lax.broadcasted_iota(jnp.int32, (1, 256), 1)
     my_count = jnp.sum(jnp.where(holders == me, counts, 0.0), axis=1, keepdims=True)
     live = lax.broadcasted_iota(jnp.int32, (3, WIDTH), 0).astype(f32) < my_count
-    slot_grad = jnp.where(live, own_grad, 0.0) * clip_scale
-    m = beta_one * first[...] + (1.0 - beta_one) * slot_grad
-    v = beta_two * second[...] + (1.0 - beta_two) * slot_grad * slot_grad
-    first_hat = m / (1.0 - beta_one**STEP)
-    second_hat = v / (1.0 - beta_two**STEP)
-    step = first_hat / (jnp.sqrt(second_hat) + adam_eps) + decay_rate * master[...]
-    w = master[...] - learn_rate * step
-    w = jnp.where(live, w, 0.0)
-    new_master[...] = w
+    w, m, v, step = update(jnp.where(live, own_grad, 0.0) * clip_scale, master[...], first[...], second[...])
+    new_master[...] = jnp.where(live, w, 0.0)
     new_first[...] = jnp.where(live, m, 0.0)
     new_second[...] = jnp.where(live, v, 0.0)
     direction[...] = jnp.where(live, step, 0.0)
 
-    w_full[...] = jnp.zeros_like(w_full)
-
-    @pl.when(c == 0)
-    def _():
-        w_full[0:3, :] = w
-
-    @pl.when(c == 1)
-    def _():
-        w_full[4:7, :] = w
-
-    for color in range(2):
-        for k in range(4):
-            at = (HALF_TILES * color + window_start(k)) * 128
-            w_send[color, k] = w_full[:, at:at + CHUNK]
-    for color in range(2):
-        here = x if color == 0 else y
-        stride = 16 if color == 0 else 64
-        for d in range(4):
-            to = (here + d) % 4
-            n = color * 4 + d
-            dev = me + (to - here) * stride + color - c
-            if d == 0:
-                @pl.when(c != color)
-                def _():
-                    pltpu.make_async_remote_copy(
-                        src_ref=w_send.at[color, here], dst_ref=w_got.at[here, c],
-                        send_sem=u_send.at[n], recv_sem=u_recv.at[c, d],
-                        device_id=(dev,), device_id_type=MESH).start()
-            else:
-                send(w_send.at[color, to], w_got.at[here, c], u_send.at[n], u_recv.at[c, d], dev)
-    w_got[p, c] = w_send[c, p]
-    for core in range(2):
-        for d in range(4):
-            def wait(core=core, d=d):
-                got(w_got.at[0, 0], u_send.at[0], u_recv.at[core, d])
-            if d == 0:
-                pl.when(c != core)(wait)
-            else:
-                wait()
-    rows = jnp.concatenate([w_got[k, 0] + w_got[k, 1] for k in range(4)], axis=0)
-    place = pl.multiple_of(q * 256 + z * 32, 32)
-    e_all[pl.ds(place, 32), :] = rows.astype(bf16)
-
-    for d in range(1, 8):
-        to = (z + d) % 8
-        send(e_all.at[pl.ds(place, 32)], e_all.at[pl.ds(place, 32)],
-             zg_send.at[d], zg_recv.at[d], me + (to - z) * 2)
     for d in range(1, 8):
         came = pl.multiple_of(q * 256 + ((z + 8 - d) % 8) * 32, 32)
         got(e_all.at[pl.ds(came, 32)], zg_send.at[d], zg_recv.at[d])
 
-    def ring_gather(part_of, pos, ssem, rsem, nxt, prv, after=None):
-        def push(k, h, s, dev):
-            send(part_of(k, h), part_of(k, h), ssem.at[s], rsem.at[s], dev)
-
-        def come(k, h, s):
-            got(part_of(k, h), ssem.at[s], rsem.at[s])
-
-        push(pos, 0, 0, prv)
-        push(pos, 1, 1, nxt)
-        push(pos, 1, 2, prv)
-        push(pos, 0, 3, nxt)
+    def ring_gather(part_of, half, pos, ssem, rsem, nxt, prv, after=None):
+        quarter = half // 2
+        above, below, far = (pos + 1) % 4, (pos + 3) % 4, (pos + 2) % 4
+
+        def push(k, at, size, s, dev):
+            send(part_of(k, at, size), part_of(k, at, size), ssem.at[s], rsem.at[s], dev)
+
+        def come(k, at, size, s):
+            got(part_of(k, at, size), ssem.at[s], rsem.at[s])
+
+        for n in range(2):
+            push(pos, n * quarter, quarter, n, prv)
+            push(pos, half + n * quarter, quarter, 2 + n, nxt)
+        push(pos, half, half, 4, prv)
+        push(pos, 0, half, 5, nxt)
         if after is not None:
-            after(pos)
-        above, below, far = (pos + 1) % 4, (pos + 3) % 4, (pos + 2) % 4
-        come(above, 0, 0)
-        push(above, 0, 4, prv)
-        come(below, 1, 1)
-        push(below, 1, 5, nxt)
-        come(above, 1, 2)
+            after(pos, 0, 2 * half)
+        for n in range(2):
+            come(above, n * quarter, quarter, n)
+            push(above, n * quarter, quarter, 6 + n, prv)
+            come(below, half + n * quarter, quarter, 2 + n)
+            push(below, half + n * quarter, quarter, 8 + n, nxt)
+        come(above, half, half, 4)
         if after is not None:
-            after(above)
-        come(below, 0, 3)
+            after(above, 0, 2 * half)
+        come(below, 0, half, 5)
         if after is not None:
-            after(below)
-        come(far, 0, 4)
-        come(far, 1, 5)
-        if after is not None:
-            after(far)
-
-    ring_gather(lambda k, h: e_all.at[pl.ds(pl.multiple_of(k * 256 + h * 128, 128), 128)],
-                q, qg_send, qg_recv, at_q((q + 1) % 4), at_q((q + 3) % 4))
+            after(below, 0, 2 * half)
+        for n in range(2):
+            come(far, n * quarter, quarter, 6 + n)
+            if after is not None:
+                after(far, n * quarter, quarter)
+            come(far, half + n * quarter, quarter, 8 + n)
+            if after is not None:
+                after(far, half + n * quarter, quarter)
+
+    ring_gather(lambda k, at, size: e_all.at[pl.ds(pl.multiple_of(k * 256 + at, 64), size)],
+                128, q, qg_send, qg_recv, at_q((q + 1) % 4), at_q((q + 3) % 4))
 
     def take_step(i, carry):
         at = pl.multiple_of(i * 128, 128)
@@ -426,34 +455,20 @@
 
     lax.fori_loop(0, 3, take_step, 0)
 
-    order = []
-
-    def pass_on(k):
-        n = len(order)
-        order.append(k)
-        send(flat_own.at[k], flat_pair.at[k], c_send.at[n], c_recv.at[n], other)
-
-    ring_gather(lambda k, h: flat_own.at[k, pl.ds(h * 192, 192)],
-                p, pg_send, pg_recv, at_p((p + 1) % 4), at_p((p + 3) % 4), pass_on)
-    stores = []
-
-    def store(buf, color, k, n):
-        at = pl.multiple_of((HALF_TILES * color + window_start(k)) * 128, 128)
-        width = OWN_TILES[k] * 128
-        copy = pltpu.make_async_copy(
-            buf.at[k, :, pl.ds(0, width)], weights.at[:, pl.ds(at, width)], out_sem.at[n])
-        copy.start()
-        stores.append(copy)
-
-    for k in range(4):
-        store(flat_own, c, k, k)
-    for n, d in enumerate((0, 1, 3, 2)):
-        got(flat_pair.at[(q + d) % 4], c_send.at[n], c_recv.at[n])
-    for k in range(4):
-        store(flat_pair, 1 - c, k, 4 + k)
-
-    for copy in stores:
-        copy.wait()
+    passed = []
+
+    def pass_on(k, at, size):
+        n = len(passed)
+        passed.append((at, size))
+        rows = pl.ds(at, size)
+        send(flat_own.at[k, rows], flat_pair.at[k, rows], c_send.at[n], c_recv.at[n], other)
+
+    ring_gather(lambda k, at, size: flat_own.at[k, pl.ds(at, size)],
+                192, p, pg_send, pg_recv, at_p((p + 1) % 4), at_p((p + 3) % 4), pass_on)
+    for n, (at, size) in enumerate(passed):
+        d = (0, 1, 3, 2, 2, 2, 2)[n]
+        got(flat_pair.at[(q + d) % 4, pl.ds(at, size)], c_send.at[n], c_recv.at[n])
+
     for copy in sends:
         copy.wait_send()
     for core in range(2):
@@ -464,22 +479,47 @@
                 send_sem=t_send.at[core * 4], recv_sem=t_recv.at[0, 0],
                 device_id=(other,), device_id_type=MESH).wait_send()
             pltpu.make_async_remote_copy(
-                src_ref=w_send.at[0, 0], dst_ref=w_got.at[0, 0],
+                src_ref=s_send.at[0, 0], dst_ref=s_got.at[0, 0],
                 send_sem=u_send.at[core * 4], recv_sem=u_recv.at[0, 0],
                 device_id=(other,), device_id_type=MESH).wait_send()
 
 
+def write(new_master, new_first, new_second, direction, flat_own, flat_pair,
+          master_out, first_out, second_out, direction_out, weights, sem):
+    c = lax.axis_index("dp") % 2
+    copies = [
+        pltpu.make_async_copy(src, dst, sem.at[8 + n])
+        for n, (src, dst) in enumerate(
+            ((new_master, master_out), (new_first, first_out), (new_second, second_out), (direction, direction_out)))
+    ]
+    for n, (buf, color) in enumerate(((flat_own, c), (flat_pair, 1 - c))):
+        for k in range(4):
+            at = pl.multiple_of((HALF_TILES * color + window_start(k)) * 128, 128)
+            width = OWN_TILES[k] * 128
+            copies.append(pltpu.make_async_copy(
+                buf.at[k, :, pl.ds(0, width)], weights.at[:, pl.ds(at, width)], sem.at[4 * n + k]))
+    for copy in copies:
+        copy.start()
+    for copy in copies:
+        copy.wait()
+
+
 def per_device(gradients, owned_rows, master, first_moment, second_moment):
     vmem = pl.BlockSpec(memory_space=pltpu.VMEM)
-    hbm = pl.BlockSpec(memory_space=pl.ANY)
+    hbm = pl.BlockSpec(memory_space=pltpu.HBM)
     state = jax.ShapeDtypeStruct(master.shape, f32)
+    flat = jax.ShapeDtypeStruct((4, ROWS, CHUNK), bf16)
     dma = pltpu.SemaphoreType.DMA
-    return pl.pallas_call(
+    results = pl.pallas_call(
         kernel,
-        out_shape=(state, state, state, state, jax.ShapeDtypeStruct((ROWS, WIDTH), bf16)),
-        in_specs=[hbm, vmem, vmem, vmem, vmem],
-        out_specs=(vmem, vmem, vmem, vmem, hbm),
+        out_shape=(state, state, state, state, flat, flat),
+        in_specs=[hbm] * 5,
+        out_specs=(vmem,) * 6,
         scratch_shapes=[
+            pltpu.VMEM((1, 256), jnp.int32),
+            pltpu.VMEM(master.shape, f32),
+            pltpu.VMEM(master.shape, f32),
+            pltpu.VMEM(master.shape, f32),
             pltpu.VMEM((4, ROWS, CHUNK), bf16),
             pltpu.VMEM((4, ROWS, CHUNK), bf16),
             pltpu.VMEM((4, ROWS, CHUNK), bf16),
@@ -504,30 +544,35 @@
             pltpu.VMEM((8, 128), f32),
             pltpu.VMEM((2, 4, 8, CHUNK), f32),
             pltpu.VMEM((8, WIDTH), f32),
-            pltpu.VMEM((8, WIDTH), f32),
-            pltpu.VMEM((2, 4, 8, CHUNK), f32),
-            pltpu.VMEM((4, 2, 8, CHUNK), f32),
+            pltpu.VMEM((24, WIDTH), f32),
+            pltpu.VMEM((2, 4, 24, CHUNK), f32),
+            pltpu.VMEM((4, 2, 24, CHUNK), f32),
             pltpu.VMEM((SLOTS, CHUNK), bf16),
-            pltpu.VMEM((4, ROWS, CHUNK), bf16),
-            pltpu.VMEM((4, ROWS, CHUNK), bf16),
-            dma((8,)),
+            dma((12,)),
             dma((4,)), dma((4,)),
-            dma((6,)), dma((6,)),
-            dma((6,)), dma((6,)),
+            dma((10,)), dma((10,)),
+            dma((10,)), dma((10,)),
             dma((8,)), dma((8,)),
             dma((8,)), dma((2, 4)),
             dma((16,)), dma((16,)),
             dma((16,)), dma((16,)),
             dma((8,)), dma((2, 4)),
             dma((8,)), dma((8,)),
-            dma((6,)), dma((6,)),
-            dma((6,)), dma((6,)),
-            dma((4,)), dma((4,)),
-            dma((8,)),
+            dma((10,)), dma((10,)),
+            dma((10,)), dma((10,)),
+            dma((7,)), dma((7,)),
         ],
         compiler_params=pltpu.CompilerParams(
             collective_id=0, has_side_effects=True, vmem_limit_bytes=48 * 1024 * 1024),
-    )(gradients, owned_rows.reshape(1, -1), master, first_moment, second_moment)
+    )(*[pltpu.with_memory_space_constraint(v, pltpu.HBM) for v in (gradients, owned_rows.reshape(1, -1), master, first_moment, second_moment)])
+    return pl.pallas_call(
+        write,
+        out_shape=(state, state, state, state, jax.ShapeDtypeStruct((ROWS, WIDTH), bf16)),
+        in_specs=[vmem] * 6,
+        out_specs=(hbm,) * 5,
+        scratch_shapes=[dma((12,))],
+        compiler_params=pltpu.CompilerParams(vmem_limit_bytes=65536),
+    )(*results)
 
 
 def solution(mesh):

time: 102 us -> 89.1 us (0.87)
  local copies, waits for them, and re-layouts: 7.65 us -> 0 us
  Pallas kernels: 93 us -> 88.4 us
    unnamed x13 -> x0, local copies, waits for them, and re-layouts: 7.65 us -> none
    pallas_call x1 -> x2, Pallas kernels: 93 us -> 88.4 us  [the longest x1 86.4 us: per_device(): pl.pallas_call(kernel, out_shape=(state, state, state, state, flat, flat)...]
where the time goes in v2:
time: 89.1 us; the launch traced here: 89 us
  Pallas kernels  88.4 us (99%)
    pallas_call x1, Pallas kernels, per_device(): pl.pallas_call(kernel, out_shape=(state, state, state, state, flat, flat)...  86.4 us
    pallas_call x1, Pallas kernels, per_device(): pl.pallas_call(write, out_shape=(state, state, state, state, jax.ShapeDty...  1.99 us

profile of v2, /device:TPU:1, one launch (start us, length us, event | category | flops | bytes accessed | tf_op | source)
XLA Modules:
  0.0 89.0 jit_solution(17405684414516567721)
XLA Ops:
  0.6 86.4 %shard_map.92 = (f32[3,4608]{1,0:T(4,128)S(1)}, f32[3,4608]{1,0:T(4,128)S(1)}, f32[3,4608]{1,0:T(4,128)S(1)}, f32[3,4608]{1,0:T(4,128)S(1)}, bf16[4,384,640]{2,1...) custom-call(bf16[1,384,4608]{2,1,0:T(8,128)(2,1)} %grad.1, s32[1,256]{1,0:T(1,128)} %bitcast.1, f32[3,4608]{1,0:T(4,128)} %master_hbm.1, ...), custom_call_target="tpu_custom_call" | custom-call | tf_op jit(solution)/shard_map/pallas_call | solution.py:513
  87.0 2.0 %shard_map.93 = (f32[3,4608]{1,0:T(4,128)}, f32[3,4608]{1,0:T(4,128)}, f32[3,4608]{1,0:T(4,128)}, f32[3,4608]{1,0:T(4,128)}, bf16[384,4608]{1,0:T(8,128)(2,1)}) custom-call(f32[3,4608]{1,0:T(4,128)S(1)} %get-tuple-element.11.new_master, f32[3,4608]{1,0:T(4,128)S(1)} %get-tuple-element.12.new_first, f32[3,4608]{1,0:T(4,128)S(1)} %get-tuple-element.13.new_second, ...), custom_call_target="tpu_custom_call" | custom-call | tf_op jit(solution)/shard_map/pallas_call | solution.py:568
